TPU v7x, 64 devices: a 2x2x8 block of a 4x4x8 slice. The times are simulated.
64 devices in a mesh: replica: 4 (over x, y), ep: 16 (over z, core).
Axes of the slice: x: 2, y: 2, z: 8, core: 2. Of those that a mesh axis runs over, the one named last changes fastest.
The devices are a block of a 4x4x8 slice.
Arguments:
- tok_in: bfloat16 [8192, 1536], P(('replica', 'ep')), parts along dimension 0
- routes: int32 [2, 8192, 8], P(None, ('replica', 'ep')), parts along dimension 1
- gate_vals: float32 [2, 8192, 8], P(None, ('replica', 'ep')), parts along dimension 1
- w_gate: bfloat16 [2, 64, 1536, 512], P(None, ('replica', 'ep')), parts along dimension 1
- w_up: bfloat16 [2, 64, 1536, 512], P(None, ('replica', 'ep')), parts along dimension 1
- w_down: bfloat16 [2, 64, 512, 1536], P(None, ('replica', 'ep')), parts along dimension 1
- sh_gate: bfloat16 [2, 1536, 512], replicated
- sh_up: bfloat16 [2, 1536, 512], replicated
- sh_down: bfloat16 [2, 512, 1536], replicated
- old_map: int32 [2, 64], P(None, 'replica'), parts along dimension 1
- move_slot: int32 [2, 16], P(None, 'replica'), parts along dimension 1
- move_expert: int32 [2, 16], P(None, 'replica'), parts along dimension 1
Outputs:
- output 1: bfloat16 [8192, 1536], P(('replica', 'ep')), parts along dimension 0
- output 2: bfloat16 [2, 64, 1536, 512], P(None, ('replica', 'ep')), parts along dimension 1
- output 3: bfloat16 [2, 64, 1536, 512], P(None, ('replica', 'ep')), parts along dimension 1
- output 4: bfloat16 [2, 64, 512, 1536], P(None, ('replica', 'ep')), parts along dimension 1
There are 4 independent parts. A program takes and returns all parts, laid end to end along the dimension named above; an argument that names none is the same for every part.
All inputs are finite; a program needn't handle non-finite values.
Results may differ from a plain program's by a relative error of at most 0.00277.
Values are sent between devices in bfloat16 or wider.
A program may use at most 768 MiB of HBM per device.

v0:
```python
import functools
import jax
import jax.numpy as jnp
from jax import lax
from jax.experimental import pallas as pl
from jax.experimental.pallas import tpu as pltpu
from jax.sharding import PartitionSpec as P

TOKEN_AXES = ('replica', 'ep')
MESH = pl.DeviceIdType.MESH
ANY = pl.BlockSpec(memory_space=pl.ANY)
VM = pl.BlockSpec(memory_space=pltpu.VMEM)
SM = pl.BlockSpec(memory_space=pltpu.SMEM)

CHUNK = 16
HOP_LAG = 5
OUT_LAG = 2
SLOTS = 48
PARTS = 4
FAST_BUSES, FAST_REACH = (4, 5), 6


def sel(pred, a, b):
    return lax.select_n(pred, b, a)


def plan_kernel(chips, me_ref, old_ref, ms_ref, mx_ref, fast_in, fast_out, slow_in, slow_out, level_ref, serve_ref):
    layers, slots = old_ref.shape
    moves = ms_ref.shape[1]
    full = layers * moves
    me = me_ref[0]
    my_core, my_chip = me & 1, lax.shift_right_logical(me, 1)

    def wrap(x):
        return x & (chips - 1) if chips & (chips - 1) == 0 else lax.rem(x, chips)

    for layer in range(layers):
        held = [old_ref[layer, q] for q in range(slots)]
        for q in range(slots):
            again = jnp.bool_(False)
            for p in range(q):
                again = again | (held[p] == held[q])
            serve_ref[layer, q] = jnp.where(again, -1, held[q])
    for ref in (fast_in, slow_in):
        for a in range(ref.shape[0]):
            for b in range(ref.shape[1]):
                ref[a, b] = 0
    for ref in (fast_out, slow_out):
        for a in range(ref.shape[0]):
            ref[a] = 0
    ring = (1 << chips) - 1

    def arc(start, dist, sign):
        run = lax.shift_left(1, dist) - 1
        low = start if sign > 0 else wrap(start - dist + 1 + chips)
        turned = lax.shift_left(run, low)
        return (turned | lax.shift_right_logical(turned, chips)) & ring

    routes = []
    for n in range(full):
        layer, i = divmod(n, moves)
        want, tgt = mx_ref[layer, i], ms_ref[layer, i]
        tgt_chip = lax.shift_right_logical(tgt, 1)
        best_key, src = jnp.int32(1 << 20), jnp.int32(0)
        for q in range(slots):
            fwd = wrap(tgt_chip - q // 2 + chips)
            key = jnp.minimum(fwd, chips - fwd)
            better = (old_ref[layer, q] == want) & (key < best_key)
            best_key = jnp.where(better, key, best_key)
            src = jnp.where(better, q, src)
        start = lax.shift_right_logical(src, 1)
        fwd = wrap(tgt_chip - start + chips)
        dists = (fwd, chips - fwd)
        bits = (arc(start, dists[0], 1), arc(start, dists[1], -1))
        routes.append((src, tgt, fwd == 0, dists, bits))

    def attempt(order, buses):
        used = [[jnp.int32(0)] * buses for _ in range(2)]
        picks, fits = {}, jnp.bool_(True)
        for half in range(2):
            for n in order:
                _, _, near, dists, bits = routes[n]
                found = []
                for lane in range(2):
                    bus = jnp.int32(buses)
                    for b in reversed(range(buses)):
                        bus = jnp.where((used[lane][b] & bits[lane]) == 0, b, bus)
                    found.append(jnp.where(dists[lane] > FAST_REACH, buses, bus))
                second = found[1] * 2 * chips + dists[1] < found[0] * 2 * chips + dists[0]
                bus = jnp.where(second, found[1], found[0])
                fits = fits & (near | (bus < buses))
                for lane in range(2):
                    mine = jnp.logical_not(near) & (second if lane == 1 else jnp.logical_not(second))
                    for b in range(buses):
                        used[lane][b] = used[lane][b] | jnp.where(mine & (bus == b), bits[lane], 0)
                picks[n, half] = (second.astype(jnp.int32), bus)
        return picks, fits

    evens, odds = list(range(0, full, 2)), list(range(1, full, 2))
    straight = list(range(full))
    orders = [straight, straight[::-1], straight[full // 2:] + straight[:full // 2], odds + evens]
    picks, level = attempt(straight, FAST_BUSES[1])
    level = jnp.where(level, 1, 2)
    for order in orders:
        other, fits = attempt(order, FAST_BUSES[0])
        for key in picks:
            picks[key] = tuple(jnp.where(fits, new, old) for new, old in zip(other[key], picks[key]))
        level = jnp.where(fits, 0, level)
    level_ref[...] = jnp.full(level_ref.shape, level, jnp.int32)

    def emit(in_ref, out_ref, lane, bus, dist, n, half, on):
        src, tgt = routes[n][:2]
        piece = 2 * (n // moves) + half

        @pl.when(on & (my_core == lane) & (my_chip == lax.shift_right_logical(src, 1)))
        def _():
            in_ref[bus, 0] = 1
            in_ref[bus, 1] = ((src & 1) != my_core).astype(jnp.int32)
            in_ref[bus, 2] = piece
            in_ref[bus, 3] = dist

        @pl.when(on & (tgt == me))
        def _():
            out_ref[piece] = jnp.where(my_core == lane, 2 + bus, 2 + full + bus)

    for n in range(full):
        src, tgt, near, dists, _ = routes[n]
        for half in range(2):
            lane, bus = picks[n, half]
            ok = jnp.logical_not(near) & (bus < FAST_BUSES[1])
            emit(fast_in, fast_out, lane, bus, jnp.where(lane == 1, dists[1], dists[0]), n, half, ok)
            emit(slow_in, slow_out, half, n, dists[half], n, half, jnp.logical_not(near))

            @pl.when(near & (tgt == me))
            def _():
                fast_out[2 * (n // moves) + half] = 1
                slow_out[2 * (n // moves) + half] = 1


def plan_moves(me, old_map, move_slot, move_expert, chips):
    layers, moves = move_slot.shape
    full = layers * moves
    i32 = jnp.int32
    return pl.pallas_call(
        functools.partial(plan_kernel, chips),
        out_shape=(jax.ShapeDtypeStruct((FAST_BUSES[1], 4), i32), jax.ShapeDtypeStruct((2 * layers,), i32),
                   jax.ShapeDtypeStruct((full, 4), i32), jax.ShapeDtypeStruct((2 * layers,), i32),
                   jax.ShapeDtypeStruct((8, 128), i32), jax.ShapeDtypeStruct(old_map.shape, i32)),
        in_specs=[SM] * 4, out_specs=(SM,) * 4 + (VM, SM),
    )(me, old_map, move_slot, move_expert)


def bus_kernel(axis_size, buses, reach, full, in_tab, out_tab, wg, wu, wd, ng, nu, nd, *scratch):
    owns, pars = scratch[:PARTS], scratch[PARTS:2 * PARTS]
    recv, send, prx, load_sem, dsend, drecv, send_sem, recv_sem, push_sem, prx_sem = scratch[2 * PARTS:]
    me = lax.axis_index('ep')
    core = lax.rem(me, 2)
    step_dir = 2 - 4 * core
    nxt = lax.rem(me + step_dir + axis_size, axis_size)
    prv = lax.rem(me - step_dir + axis_size, axis_size)
    mate = me + 1 - 2 * core
    layers, tall, width = wg.shape[0], wg.shape[1], wg.shape[3]
    low, blocks = wd.shape[1], wd.shape[3] // width
    half_chunks = (2 * tall + blocks * low) // 2
    span = half_chunks // PARTS

    def pieces(part, g, u, d):
        out = []
        for layer in range(layers):
            areas = [(g.at[layer], 0, tall), (u.at[layer], tall, tall)]
            areas += [(d.at[layer, :, :, pl.ds(n * width, width)], 2 * tall + n * low, low) for n in range(blocks)]
            for half in range(2):
                lo = half * half_chunks + part * span
                for ref, at, size in areas:
                    first, last = max(lo, at), min(lo + span, at + size)
                    if first < last:
                        out.append((ref.at[pl.ds(first - at, last - first)], (2 * layer + half) * span + first - lo, last - first))
        return out

    def local_copies(part, refs, out):
        copies = []
        for n, (ref, at, size) in enumerate(pieces(part, *refs)):
            here = owns[part].at[pl.ds(at, size)]
            copies.append(pltpu.make_async_copy(*((here, ref) if out else (ref, here)), load_sem.at[part, n]))
        return copies

    def share(part):
        return pltpu.make_async_remote_copy(owns[part], pars[part], dsend.at[part], drecv.at[part],
                                            device_id={'ep': mate}, device_id_type=MESH)

    def ring_copy(slot):
        return pltpu.make_async_remote_copy(send.at[slot], recv.at[slot], send_sem.at[slot], recv_sem.at[slot],
                                            device_id={'ep': nxt}, device_id_type=MESH)

    def push_copy(slot):
        return pltpu.make_async_remote_copy(recv.at[slot], prx.at[slot], push_sem.at[slot], prx_sem.at[slot],
                                            device_id={'ep': mate}, device_id_type=MESH)

    for copy in local_copies(0, (wg, wu, wd), False):
        copy.start()
    barrier = pltpu.get_barrier_semaphore()
    for peer in (nxt, prv, mate):
        pl.semaphore_signal(barrier, inc=1, device_id={'ep': peer}, device_id_type=MESH)
    pl.semaphore_wait(barrier, 3)
    for part in range(PARTS):
        for copy in local_copies(part, (wg, wu, wd), False):
            copy.wait()
        share(part).start()
        if part == 0:
            for later in range(1, PARTS):
                for copy in local_copies(later, (wg, wu, wd), False):
                    copy.start()

    sends = half_chunks + (reach - 1) * HOP_LAG
    first_out = reach * HOP_LAG
    first_store = first_out + OUT_LAG
    total = first_store + half_chunks
    edges = {0, HOP_LAG, sends, sends + HOP_LAG, first_out, first_out + half_chunks, total}
    edges |= {p * span for p in range(PARTS + 1)} | {first_store + p * span for p in range(PARTS)}
    edges = sorted(edges)

    for begin, end in zip(edges[:-1], edges[1:]):
        lead = min(begin // span, PARTS - 1)
        if begin % span == 0 and begin < half_chunks:
            share(lead).wait()
        done = (begin - first_store) // span
        if begin >= first_store and (begin - first_store) % span == 0 and done > 0:
            for copy in local_copies(done - 1, (ng, nu, nd), True):
                copy.start()

        def step(t, carry, begin=begin, lead=lead, done=done):
            slot = lax.rem(t, SLOTS)
            old_slot = lax.rem(t - HOP_LAG + SLOTS, SLOTS)
            if HOP_LAG <= begin < sends + HOP_LAG:
                ring_copy(old_slot).wait()
            if begin < sends:
                for j in range(buses):
                    pick = t - (reach - in_tab[j, 3]) * HOP_LAG
                    at = in_tab[j, 2] * span
                    late = at + jnp.minimum(jnp.maximum(pick - lead * span, 0), span - 1)
                    mine, theirs = owns[lead][late], pars[lead][late]
                    if lead > 0:
                        early = at + jnp.minimum(jnp.maximum(pick - (lead - 1) * span, 0), span - 1)
                        fresh = pick >= lead * span
                        mine = sel(fresh, mine, owns[lead - 1][early])
                        theirs = sel(fresh, theirs, pars[lead - 1][early])
                    value = sel(in_tab[j, 1] != 0, theirs, mine)
                    if begin >= HOP_LAG:
                        value = sel(in_tab[j, 0] != 0, value, recv[old_slot, j])
                    send[slot, j] = value
                ring_copy(slot).start()
            if first_out <= begin < first_out + half_chunks:
                push_copy(old_slot).start()
            if begin >= first_store:
                k = t - first_store - done * span
                src = lax.rem(t - OUT_LAG - HOP_LAG + SLOTS, SLOTS)
                push_copy(src).wait()
                for piece in range(2 * layers):
                    code = out_tab[piece]
                    at = piece * span + k
                    value = sel(code == 1, pars[done][at], owns[done][at])
                    for j in range(buses):
                        value = sel(code == 2 + j, recv[src, j], value)
                        value = sel(code == 2 + full + j, prx[src, j], value)
                    owns[done][at] = value
            return carry

        lax.fori_loop(begin, end, step, 0)

    for copy in local_copies(PARTS - 1, (ng, nu, nd), True):
        copy.start()
    for part in range(PARTS):
        for copy in local_copies(part, (ng, nu, nd), True):
            copy.wait()


def move_weights(axis_size, buses, reach, full, cid, in_tab, out_tab, *weights):
    cut = [w.reshape(w.shape[0], w.shape[2] // CHUNK, CHUNK, w.shape[3]) for w in weights]
    layers, tall, _, width = cut[0].shape
    low, blocks = cut[2].shape[1], cut[2].shape[3] // width
    bf16 = jnp.bfloat16
    dma = pltpu.SemaphoreType.DMA
    ring = pltpu.VMEM((SLOTS, buses, CHUNK, width), bf16)
    part = pltpu.VMEM((layers * (2 * tall + blocks * low) // PARTS, CHUNK, width), bf16)
    out = pl.pallas_call(
        functools.partial(bus_kernel, axis_size, buses, reach, full),
        out_shape=tuple(jax.ShapeDtypeStruct(w.shape, bf16) for w in cut),
        in_specs=[SM, SM, ANY, ANY, ANY], out_specs=(ANY,) * 3,
        scratch_shapes=[part] * (2 * PARTS) + [ring, ring, ring,
                        dma((PARTS, 4 * layers)), dma((PARTS,)), dma((PARTS,)),
                        dma((SLOTS,)), dma((SLOTS,)), dma((SLOTS,)), dma((SLOTS,))],
        compiler_params=pltpu.CompilerParams(collective_id=cid, has_side_effects=True, vmem_limit_bytes=(42 if buses > 5 else 34) * 1024 * 1024),
    )(in_tab, out_tab, *cut)
    return tuple(n.reshape(w.shape) for n, w in zip(out, weights))


def new_layout(axis_size, plan, level, *weights):
    fast_in, fast_out, slow_in, slow_out = plan[:4]
    full = slow_in.shape[0]

    def fast(buses, cid):
        return lambda *w: move_weights(axis_size, buses, FAST_REACH, full, cid, fast_in, fast_out, *w)

    def slow(*w):
        return move_weights(axis_size, full, axis_size // 2 - 1, full, 3, slow_in, slow_out, *w)

    return lax.switch(level, (fast(FAST_BUSES[0], 1), fast(FAST_BUSES[1], 2), slow), *weights)


SUBS = 2


def token_kernel(axis_size, groups, tok, gt, flag, wg, wu, wd, sg, su, sd, out, any_flag,
                 xb, rs, pp, pst, first, home, gbuf, fbuf, eg, eu, ed, hg, hu, hd,
                 w_sem, s_sem, g_send, g_recv, x_send, x_recv, m_send, m_recv, p_send, p_recv, r_send, r_recv, f_send, f_recv):
    me = lax.axis_index('ep')
    core, chip = lax.rem(me, 2), lax.div(me, 2)
    chips = axis_size // 2
    step_dir = 2 - 4 * core
    nxt = lax.rem(me + step_dir + axis_size, axis_size)
    mate = me + 1 - 2 * core
    layers = wg.shape[0]
    rows, width = tok.shape
    hops = chips - 1
    cols = wg.shape[2]

    def shared_loads(layer):
        return [pltpu.make_async_copy(a.at[layer], b, s_sem.at[n]) for n, (a, b) in enumerate(((sg, hg), (su, hu), (sd, hd)))]

    def expert_loads(layer):
        return [pltpu.make_async_copy(a.at[layer], b.at[layer], w_sem.at[3 * layer + n])
                for n, (a, b) in enumerate(((wg, eg), (wu, eu), (wd, ed)))]

    for copy in shared_loads(0) + expert_loads(0):
        copy.start()
    barrier = pltpu.get_barrier_semaphore()
    for off in range(1, axis_size):
        pl.semaphore_signal(barrier, inc=1, device_id={'ep': lax.rem(me + off, axis_size)}, device_id_type=MESH)
    group = lax.axis_index('replica')
    for off in range(1, groups):
        pl.semaphore_signal(barrier, inc=1, device_id={'replica': lax.rem(group + off, groups)}, device_id_type=MESH)
    pl.semaphore_wait(barrier, axis_size + groups - 2)

    def token_copy(src_slot, dst_slot, sub):
        piece = pl.ds(sub * (rows // SUBS), rows // SUBS)
        return pltpu.make_async_remote_copy(xb.at[src_slot, core, piece], xb.at[dst_slot, core, piece],
                                            x_send.at[dst_slot, sub], x_recv.at[dst_slot, sub],
                                            device_id={'ep': nxt}, device_id_type=MESH)

    def mate_copy(slot):
        return pltpu.make_async_remote_copy(xb.at[slot, core], xb.at[slot, core], m_send.at[slot], m_recv.at[slot],
                                            device_id={'ep': mate}, device_id_type=MESH)

    def mate_arrival(slot):
        other = 1 - core
        return pltpu.make_async_remote_copy(xb.at[slot, other], xb.at[slot, other], m_send.at[slot], m_recv.at[slot],
                                            device_id={'ep': mate}, device_id_type=MESH)

    def part_copy(stage, slot, c):
        blk = pl.ds(c * cols, cols)
        return pltpu.make_async_remote_copy(pst.at[stage, 1 - core, :, blk], pp.at[slot, :, blk], p_send.at[stage, c], p_recv.at[slot, c],
                                            device_id={'ep': mate}, device_id_type=MESH)

    def sum_copy(src, at, slot, sub):
        piece = pl.ds(sub * (rows // SUBS), rows // SUBS)
        return pltpu.make_async_remote_copy(src.at[at, piece], rs.at[slot, piece], r_send.at[slot, sub], r_recv.at[slot, sub],
                                            device_id={'ep': nxt}, device_id_type=MESH)

    xb[hops, core] = tok[...]
    for sub in range(SUBS):
        token_copy(hops, 0, sub).start()
    mate_copy(hops).start()

    def gate_copy(off):
        peer = lax.rem(me + off, axis_size)
        return pltpu.make_async_remote_copy(gt.at[peer], gbuf.at[me], g_send.at[off], g_recv.at[off],
                                            device_id={'ep': peer}, device_id_type=MESH)

    def gate_arrival(off):
        peer = lax.rem(me - off + axis_size, axis_size)
        return pltpu.make_async_remote_copy(gt.at[peer], gbuf.at[peer], g_send.at[off], g_recv.at[off],
                                            device_id={'ep': peer}, device_id_type=MESH)

    for off in range(1, axis_size):
        gate_copy(off).start()
    gbuf[me] = gt[me]

    def flag_copy(off):
        peer = lax.rem(group + off, groups)
        return pltpu.make_async_remote_copy(flag, fbuf.at[off], f_send.at[off], f_recv.at[off],
                                            device_id={'replica': peer}, device_id_type=MESH)

    for off in range(1, groups):
        flag_copy(off).start()
    fbuf[0] = flag[...]

    def inner(x, w_gate, w_up):
        gate_proj = jnp.dot(x, w_gate, preferred_element_type=jnp.float32)
        up_proj = jnp.dot(x, w_up, preferred_element_type=jnp.float32)
        return (jax.nn.silu(gate_proj) * up_proj).astype(jnp.bfloat16)

    def spread(src, layer):
        row = gbuf[src, pl.ds(layer, 1), :]
        return jnp.broadcast_to(row, (rows, rows)).T

    for layer in range(layers):
        base = layer * chips
        rbase = layer * hops
        own = base + hops
        for copy in shared_loads(layer):
            copy.wait()
        mine = xb[own, core]
        act = inner(mine, hg[...], hu[...])
        for c in range(width // cols):
            blk = pl.ds(c * cols, cols)
            home[:, blk] = xb[own, core, :, blk].astype(jnp.float32) + jnp.dot(act, hd[:, blk], preferred_element_type=jnp.float32)
        if layer + 1 < layers:
            for copy in shared_loads(layer + 1):
                copy.start()
        def relay(slot, onward):
            for sub in range(SUBS):
                token_copy(slot, slot, sub).wait_recv()

                @pl.when(onward)
                def _():
                    token_copy(slot, slot + 1, sub).start()
            mate_copy(slot).start()

        def partial(s):
            slot, stage = base + s, lax.rem(s, 2)
            mate_arrival(slot).wait_recv()

            @pl.when(s >= 2)
            def _():
                for c in range(width // cols):
                    part_copy(stage, slot, c).wait_send()
            x = xb[slot].reshape(2 * rows, width)
            act = inner(x, eg[layer], eu[layer])

            @pl.when(s + 1 < hops)
            def _():
                relay(slot + 1, s + 2 < hops)
            src_a = 2 * lax.rem(chip - 1 - s + 2 * chips, chips)
            src_b = 2 * lax.rem(chip + 1 + s, chips) + 1
            scale = jnp.concatenate([spread(src_a, layer), spread(src_b, layer)], axis=0)
            scale = jnp.concatenate([scale] * (cols // rows), axis=1)
            for c in range(width // cols):
                blk = pl.ds(c * cols, cols)
                y = jnp.dot(act, ed[layer, :, blk], preferred_element_type=jnp.float32) * scale
                pst[stage, 0, :, blk] = y[:rows]
                pst[stage, 1, :, blk] = y[rows:]
                part_copy(stage, slot, c).start()

        def step(s, carry):
            @pl.when(s >= 0)
            def _():
                slot, stage = base + s, lax.rem(s, 2)
                for c in range(width // cols):
                    part_copy(stage, slot, c).wait_recv()
                for sub in range(SUBS):
                    piece = pl.ds(sub * (rows // SUBS), rows // SUBS)

                    @pl.when(s == 0)
                    def _():
                        first[layer, piece] = pst[stage, core, piece] + pp[slot, piece]
                        sum_copy(first, layer, rbase, sub).start()

                    @pl.when(s > 0)
                    def _():
                        sum_copy(rs, 0, rbase + s - 1, sub).wait_recv()

                    @pl.when((s > 0) & (s < hops))
                    def _():
                        at = rbase + s - 1
                        rs[at, piece] = rs[at, piece] + pst[stage, core, piece] + pp[slot, piece]
                        sum_copy(rs, at, at + 1, sub).start()

                    @pl.when(s == hops)
                    def _():
                        total = rs[rbase + hops - 1, piece] + pst[stage, core, piece] + pp[slot, piece] + home[piece]
                        if layer + 1 < layers:
                            xb[own + chips, core, piece] = total.astype(jnp.bfloat16)
                            token_copy(own + chips, base + chips, sub).start()
                        else:
                            out[piece] = total.astype(jnp.bfloat16)

            @pl.when(s + 1 < chips)
            def _():
                partial(s + 1)
            return carry

        relay(base, True)
        for copy in expert_loads(layer):
            copy.wait()
        if layer + 1 < layers:
            for copy in expert_loads(layer + 1):
                copy.start()
        if layer == 0:
            for off in range(1, axis_size):
                gate_arrival(off).wait_recv()
        lax.fori_loop(-1, chips, step, 0)
        if layer + 1 < layers:
            mate_copy(own + chips).start()
        for stage in range(2):
            for c in range(width // cols):
                part_copy(stage, base, c).wait_send()

    for off in range(1, axis_size):
        gate_copy(off).wait_send()

    def settle(n, carry):
        layer, s = lax.div(n, chips), lax.rem(n, chips)
        mate_copy(n).wait_send()

        @pl.when(s < hops)
        def _():
            for sub in range(SUBS):
                token_copy(n, n, sub).wait_send()
                sum_copy(first, 0, layer * hops + s, sub).wait_send()
        return carry

    lax.fori_loop(0, layers * chips, settle, 0)
    for off in range(1, groups):
        flag_copy(off).wait()
    any_flag[0] = jnp.max(jnp.max(fbuf[...], axis=0))


def both_layers(axis_size, groups, cid, tok, gt, flag, wg, wu, wd, sg, su, sd):
    layers, depth, cols = wg.shape
    rows, width = tok.shape
    chips = axis_size // 2
    hops = chips - 1
    bf16, f32 = jnp.bfloat16, jnp.float32
    dma = pltpu.SemaphoreType.DMA
    full = layers * chips
    return pl.pallas_call(
        functools.partial(token_kernel, axis_size, groups),
        out_shape=(jax.ShapeDtypeStruct(tok.shape, bf16), jax.ShapeDtypeStruct((1,), flag.dtype)),
        in_specs=[VM, VM, VM] + [ANY] * 6, out_specs=(VM, SM),
        scratch_shapes=[pltpu.VMEM((full, 2, rows, width), bf16), pltpu.VMEM((layers * hops, rows, width), f32),
                        pltpu.VMEM((full, rows, width), f32), pltpu.VMEM((2, 2, rows, width), f32),
                        pltpu.VMEM((layers, rows, width), f32), pltpu.VMEM((rows, width), f32),
                        pltpu.VMEM((axis_size, layers, rows), f32), pltpu.VMEM((groups,) + flag.shape, flag.dtype),
                        pltpu.VMEM((layers, depth, cols), bf16), pltpu.VMEM((layers, depth, cols), bf16),
                        pltpu.VMEM((layers, cols, depth), bf16),
                        pltpu.VMEM((depth, cols), bf16), pltpu.VMEM((depth, cols), bf16), pltpu.VMEM((cols, depth), bf16),
                        dma((3 * layers,)), dma((3,)), dma((axis_size,)), dma((axis_size,)),
                        dma((full, SUBS)), dma((full, SUBS)), dma((full,)), dma((full,)),
                        dma((2, width // cols)), dma((full, width // cols)), dma((layers * hops, SUBS)), dma((layers * hops, SUBS)), dma((groups,)), dma((groups,))],
        compiler_params=pltpu.CompilerParams(collective_id=cid, has_side_effects=True, vmem_limit_bytes=63 * 1024 * 1024),
    )(tok, gt, flag, wg, wu, wd, sg, su, sd)


def solution(mesh):
    def body(tok_in, routes, gate_vals, w_gate, w_up, w_down, sh_gate, sh_up, sh_down, old_map, move_slot, move_expert):
        axis_size = mesh.shape['ep']
        me = lax.axis_index('ep').astype(jnp.int32)[None]
        plan = plan_moves(me, old_map, move_slot, move_expert, axis_size // 2)
        hit = routes[None] == plan[5].T[:, :, None, None]
        gates = jnp.sum(jnp.where(hit, gate_vals[None], 0.0), axis=3)
        tok_out, level = both_layers(axis_size, mesh.shape['replica'], 0, tok_in, gates, plan[4], w_gate[:, 0], w_up[:, 0], w_down[:, 0], sh_gate, sh_up, sh_down)
        placed = new_layout(axis_size, plan, level[0], w_gate, w_up, w_down)
        return (tok_out, *placed)

    weight_spec = P(None, TOKEN_AXES, None, None)
    route_spec = P(None, TOKEN_AXES, None)
    map_spec = P(None, 'replica')
    shared_spec = P(None, None, None)
    tok_spec = P(TOKEN_AXES, None)
    return jax.shard_map(body, mesh=mesh, in_specs=(tok_spec, route_spec, route_spec, weight_spec, weight_spec, weight_spec, shared_spec, shared_spec, shared_spec, map_spec, map_spec, map_spec), out_specs=(tok_spec, weight_spec, weight_spec, weight_spec), check_vma=False)
```

profile of v0, /device:TPU:21, one launch (start us, length us, event | category | flops | bytes accessed | tf_op | source)
XLA Modules:
  0.0 344.0 jit_solution(2925894076251417395)
XLA Ops:
  0.6 4.3 %shard_map.147 = (s32[5,4]{1,0:T(8,128)S(1)}, s32[4]{0:T(128)S(1)}, s32[8,4]{1,0:T(8,128)S(1)}, s32[4]{0:T(128)S(1)}, s32[8,128]{1,0:T(8,128)}, /*index=5*/s32[2,16]{1,0:T(2,128)}) custom-call(s32[1]{0:T(128)} %bitcast.27.me_ref, s32[2,16]{1,0:T(2,128)} %old_ref.1, s32[2,4]{1,0:T(2,128)} %ms_ref.1, s32[2,4]{1,0:T(2,128)} %mx_ref.1), custom_call_target="tpu_custom_call" | custom-call | tf_op jit(solution)/shard_map/pallas_call | solution.py:144
  4.9 0.8 copy.31
  5.7 1.4 select_reduce_fusion.gt
  7.1 197.0 %shard_map.148 = (bf16[128,1536]{1,0:T(8,128)(2,1)}, s32[1]{0:T(128)}) custom-call(bf16[128,1536]{1,0:T(8,128)(2,1)} %tok.1, f32[16,2,128]{2,1,0:T(2,128)} %select_reduce_fusion.gt, s32[8,128]{1,0:T(8,128)} %get-tuple-element.70.flag, bf16[2,1536,512]{2,1,0:T(8,128)(2,1)} %bitcast.42, bf16[2,1536,512]{2,1,0:T(8,128)(2,1)} %bitcast.46, ...), custom_call_target="tpu_custom_call" | custom-call | tf_op jit(solution)/shard_map/pallas_call | solution.py:536
  204.8 0.0 copy-start
  204.8 133.4 %conditional.1 = ((bf16[2,96,16,512]{3,2,1,0:T(8,128)(2,1)S(1)}, bf16[2,96,16,512]{3,2,1,0:T(8,128)(2,1)S(1)}, bf16[2,32,16,1536]{3,2,1,0:T(8,128)(2,1)S(1)})) conditional(s32[]{:T(128)} %bitcast.32, (bf16[2,1,1536,512]{3,2,1,0:T(8,128)(2,1)}, bf16[2,1,1536,512]{3,2,1,0:T(8,128)(2,1)}, bf16[2,1,512,1536]{3,2,1,0:T(8,128)(2,1)}, ...), branch_computations={%region_1.2_spmd, %region_2.3_spmd, %region_3.4_spmd} | conditional | bytes 8 | solution.py:307
  205.0 133.2 %branch_0_fun.1 = (bf16[2,96,16,512]{3,2,1,0:T(8,128)(2,1)S(1)}, bf16[2,96,16,512]{3,2,1,0:T(8,128)(2,1)S(1)}, bf16[2,32,16,1536]{3,2,1,0:T(8,128)(2,1)S(1)}) custom-call(s32[5,4]{1,0:T(8,128)S(1)} %get-tuple-element.30.in_tab, s32[4]{0:T(128)S(1)} %get-tuple-element.31.out_tab, bf16[2,96,16,512]{3,2,1,0:T(8,128)(2,1)} %bitcast.43, ...), custom_call_target="tpu_custom_call" | custom-call | tf_op jit(solution)/shard_map/cond/branch_0_fun/pallas_call | solution.py:285
  338.3 0.0 copy-done
  338.3 0.7 copy.57
  339.0 1.7 copy.58
  340.7 1.7 copy.59
  342.3 1.7 copy.60
Async XLA Ops:
  204.8 133.5 %copy-start = (bf16[128,1536]{1,0:T(8,128)(2,1)S(1)}, bf16[128,1536]{1,0:T(8,128)(2,1)}, u32[]{:S(2)}) copy-start(bf16[128,1536]{1,0:T(8,128)(2,1)} %get-tuple-element.138) | copy-start | bytes 1179652
where the time goes:
time: 344 us
  Pallas kernels  335 us (97%)
  local copies, waits for them, and re-layouts  6.5 us (2%)
    pallas_call x1, Pallas kernels, both_layers(): pl.pallas_call(functools.partial(token_kernel, axis_size, groups), out_sh...  197 us
    pallas_call x1, Pallas kernels, move_weights(): pl.pallas_call(functools.partial(bus_kernel, axis_size, buses, reach, ful...  133 us

commit v1 on v0

--- a/solution.py
+++ b/solution.py
@@ -185,8 +185,12 @@
         return copies
 
     def share(part):
-        return pltpu.make_async_remote_copy(owns[part], pars[part], dsend.at[part], drecv.at[part],
-                                            device_id={'ep': mate}, device_id_type=MESH)
+        if part > 0:
+            routes = [(owns[part], pars[part], part)]
+        else:
+            routes = [(ref, pars[0].at[pl.ds(at, size)], PARTS + n) for n, (ref, at, size) in enumerate(pieces(0, wg, wu, wd))]
+        return [pltpu.make_async_remote_copy(src, dst, dsend.at[n], drecv.at[n], device_id={'ep': mate}, device_id_type=MESH)
+                for src, dst, n in routes]
 
     def ring_copy(slot):
         return pltpu.make_async_remote_copy(send.at[slot], recv.at[slot], send_sem.at[slot], recv_sem.at[slot],
@@ -202,11 +206,14 @@
     for peer in (nxt, prv, mate):
         pl.semaphore_signal(barrier, inc=1, device_id={'ep': peer}, device_id_type=MESH)
     pl.semaphore_wait(barrier, 3)
+    for copy in share(0):
+        copy.start()
     for part in range(PARTS):
         for copy in local_copies(part, (wg, wu, wd), False):
             copy.wait()
-        share(part).start()
-        if part == 0:
+        if part > 0:
+            share(part)[0].start()
+        else:
             for later in range(1, PARTS):
                 for copy in local_copies(later, (wg, wu, wd), False):
                     copy.start()
@@ -222,7 +229,8 @@
     for begin, end in zip(edges[:-1], edges[1:]):
         lead = min(begin // span, PARTS - 1)
         if begin % span == 0 and begin < half_chunks:
-            share(lead).wait()
+            for copy in share(lead):
+                copy.wait()
         done = (begin - first_store) // span
         if begin >= first_store and (begin - first_store) % span == 0 and done > 0:
             for copy in local_copies(done - 1, (ng, nu, nd), True):
@@ -287,7 +295,7 @@
         out_shape=tuple(jax.ShapeDtypeStruct(w.shape, bf16) for w in cut),
         in_specs=[SM, SM, ANY, ANY, ANY], out_specs=(ANY,) * 3,
         scratch_shapes=[part] * (2 * PARTS) + [ring, ring, ring,
-                        dma((PARTS, 4 * layers)), dma((PARTS,)), dma((PARTS,)),
+                        dma((PARTS, 4 * layers)), dma((PARTS + 4 * layers,)), dma((PARTS + 4 * layers,)),
                         dma((SLOTS,)), dma((SLOTS,)), dma((SLOTS,)), dma((SLOTS,))],
         compiler_params=pltpu.CompilerParams(collective_id=cid, has_side_effects=True, vmem_limit_bytes=(42 if buses > 5 else 34) * 1024 * 1024),
     )(in_tab, out_tab, *cut)

time: 344 us -> 344 us (level)
  no operation moved by 1% of the time
where the time goes in v1:
time: 344 us
  Pallas kernels  334 us (97%)
  local copies, waits for them, and re-layouts  6.5 us (2%)
    pallas_call x1, Pallas kernels, both_layers(): pl.pallas_call(functools.partial(token_kernel, axis_size, groups), out_sh...  197 us
    pallas_call x1, Pallas kernels, move_weights(): pl.pallas_call(functools.partial(bus_kernel, axis_size, buses, reach, ful...  133 us

profile of v1, /device:TPU:21, one launch (start us, length us, event | category | flops | bytes accessed | tf_op | source)
XLA Modules:
  0.0 343.8 jit_solution(6691889695593233283)
XLA Ops:
  0.6 4.3 %shard_map.147 = (s32[5,4]{1,0:T(8,128)S(1)}, s32[4]{0:T(128)S(1)}, s32[8,4]{1,0:T(8,128)S(1)}, s32[4]{0:T(128)S(1)}, s32[8,128]{1,0:T(8,128)}, /*index=5*/s32[2,16]{1,0:T(2,128)}) custom-call(s32[1]{0:T(128)} %bitcast.27.me_ref, s32[2,16]{1,0:T(2,128)} %old_ref.1, s32[2,4]{1,0:T(2,128)} %ms_ref.1, s32[2,4]{1,0:T(2,128)} %mx_ref.1), custom_call_target="tpu_custom_call" | custom-call | tf_op jit(solution)/shard_map/pallas_call | solution.py:144
  4.9 0.8 copy.31
  5.7 1.4 select_reduce_fusion.gt
  7.1 197.0 %shard_map.148 = (bf16[128,1536]{1,0:T(8,128)(2,1)}, s32[1]{0:T(128)}) custom-call(bf16[128,1536]{1,0:T(8,128)(2,1)} %tok.1, f32[16,2,128]{2,1,0:T(2,128)} %select_reduce_fusion.gt, s32[8,128]{1,0:T(8,128)} %get-tuple-element.70.flag, bf16[2,1536,512]{2,1,0:T(8,128)(2,1)} %bitcast.42, bf16[2,1536,512]{2,1,0:T(8,128)(2,1)} %bitcast.46, ...), custom_call_target="tpu_custom_call" | custom-call | tf_op jit(solution)/shard_map/pallas_call | solution.py:544
  204.8 0.0 copy-start
  204.8 133.2 %conditional.1 = ((bf16[2,96,16,512]{3,2,1,0:T(8,128)(2,1)S(1)}, bf16[2,96,16,512]{3,2,1,0:T(8,128)(2,1)S(1)}, bf16[2,32,16,1536]{3,2,1,0:T(8,128)(2,1)S(1)})) conditional(s32[]{:T(128)} %bitcast.32, (bf16[2,1,1536,512]{3,2,1,0:T(8,128)(2,1)}, bf16[2,1,1536,512]{3,2,1,0:T(8,128)(2,1)}, bf16[2,1,512,1536]{3,2,1,0:T(8,128)(2,1)}, ...), branch_computations={%region_1.2_spmd, %region_2.3_spmd, %region_3.4_spmd} | conditional | bytes 8 | solution.py:315
  205.0 133.0 %branch_0_fun.1 = (bf16[2,96,16,512]{3,2,1,0:T(8,128)(2,1)S(1)}, bf16[2,96,16,512]{3,2,1,0:T(8,128)(2,1)S(1)}, bf16[2,32,16,1536]{3,2,1,0:T(8,128)(2,1)S(1)}) custom-call(s32[5,4]{1,0:T(8,128)S(1)} %get-tuple-element.30.in_tab, s32[4]{0:T(128)S(1)} %get-tuple-element.31.out_tab, bf16[2,96,16,512]{3,2,1,0:T(8,128)(2,1)} %bitcast.43, ...), custom_call_target="tpu_custom_call" | custom-call | tf_op jit(solution)/shard_map/cond/branch_0_fun/pallas_call | solution.py:293
  338.0 0.0 copy-done
  338.0 0.7 copy.57
  338.8 1.7 copy.58
  340.5 1.7 copy.59
  342.1 1.7 copy.60
Async XLA Ops:
  204.8 133.2 %copy-start = (bf16[128,1536]{1,0:T(8,128)(2,1)S(1)}, bf16[128,1536]{1,0:T(8,128)(2,1)}, u32[]{:S(2)}) copy-start(bf16[128,1536]{1,0:T(8,128)(2,1)} %get-tuple-element.138) | copy-start | bytes 1179652
